TPU v7x, 32 devices: a whole 2x2x4 slice. The times are simulated.
32 devices in a mesh: groups: 2 (over x), kv: 16 (over z, y, core).
Axes of the slice: x: 2, y: 2, z: 4, core: 2. Of those that a mesh axis runs over, the one named last changes fastest.
Arguments:
- queries: bfloat16 [80, 18432], P('groups', 'kv'), parts along dimension 0, may hold values from -240 to 240
- latent_cache: bfloat16 [80, 2048, 576], P('groups', 'kv'), parts along dimension 0, may hold values from -6 to 6
- context_lengths: int32 [80], P('groups'), parts along dimension 0, may hold values from 128 to 2048, as said below
- value_up: bfloat16 [16384, 128], P('kv'), may hold values from -0.25 to 0.25
- out_proj: bfloat16 [4096, 7168], P('kv'), may hold values from -0.09375 to 0.09375
- residual: bfloat16 [80, 7168], P('groups', 'kv'), parts along dimension 0, may hold values from -0.75 to 0.75
- norm_gain: bfloat16 [7168], P('kv'), may hold values from 0.5 to 1.5
- expert_ids: int32 [80, 8], P('groups'), parts along dimension 0, may hold values from 0 to 255, all different within a row; in each aligned block of 40 rows (0 to 39, 40 to 79, ...) at most 2 rows name the same one
- gate_weights: float32 [80, 8], P('groups'), parts along dimension 0, may hold values from 0.05 to 0.5
Outputs:
- dispatched: bfloat16 [512, 2, 7168], P(('groups', 'kv')), parts along dimension 0
- slot_scale: float32 [512, 2], P(('groups', 'kv')), parts along dimension 0
- slot_gate: float32 [512, 2], P(('groups', 'kv')), parts along dimension 0
There are 2 independent parts, one for each index of `groups`. A program takes and returns all parts, laid end to end along the dimension named above; an argument that names none is the same for every part. Nothing has to cross between parts.
Inputs may be any that keep to these rules, and one draw needn't show every extreme that they name: `context_lengths`: multiples of 128; some sequence is 2048 long. `expert_ids`: each token names 8 different experts; no expert is named by more than 2 tokens, a bound that some block reaches.
All inputs are finite; a program needn't handle non-finite values. Where the computation divides by a largest or mean magnitude, that divisor is 1e-20 or more.
Results may differ from a plain program's by a relative error of at most 0.0069.
Values may be sent and summed in bfloat16 or wider, within the bound.
A program may use at most 64 MiB of HBM per device.

v0:
```python
import jax
import jax.numpy as jnp
from jax import lax
from jax.sharding import PartitionSpec as P

H = 32
LAT = 512
ROPE = 64
VD = 128
D = 7168
EXPERTS = 256
TOPK = 8
CAP = 2
score_scale = 192.0 ** (-0.5)
masked_score = -1e30
small_eps = 1e-06


def from_partner(value, axis, bit):
    mask = 2**bit
    pairs = [(source, source ^ mask) for source in range(lax.axis_size(axis))]
    return lax.ppermute(value, axis, pairs)


def slot_targets(expert_ids):
    flat_ids = expert_ids.reshape(-1)
    order_index = jnp.arange(flat_ids.shape[0], dtype=jnp.int32)
    same_before = (flat_ids[:, None] == flat_ids[None, :]) & (
        order_index[None, :] < order_index[:, None]
    )
    rank_within = jnp.sum(same_before.astype(jnp.int32), axis=1)
    return flat_ids * CAP + rank_within


def slot_match(targets, first_slot, slot_count):
    slot_index = first_slot + jnp.arange(slot_count, dtype=jnp.int32)
    return (slot_index[:, None] == targets[None, :]).astype(jnp.float32)


def token_picker(matches, seq_count):
    return jnp.sum(matches.reshape(matches.shape[0], seq_count, TOPK), axis=2)


def per_device(
    queries,
    latent_cache,
    context_lengths,
    value_up,
    out_proj,
    residual,
    norm_gain,
    expert_ids,
    gate_weights,
):
    kv_count = lax.axis_size("kv")
    shard_index = lax.axis_index("kv")
    seq_count = queries.shape[0]
    query_rows = lax.all_gather(queries, "kv", axis=1, tiled=True).reshape(seq_count, H, LAT + ROPE)
    ctx_local = latent_cache.shape[1]
    scores = (
        jnp.einsum("shq,scq->shc", query_rows, latent_cache, preferred_element_type=jnp.float32)
        * score_scale
    )
    position = shard_index * ctx_local + jnp.arange(ctx_local, dtype=jnp.int32)
    valid_mask = (position[None, :] < context_lengths[:, None])[:, None, :]
    scores = jnp.where(valid_mask, scores, masked_score)
    local_max = jnp.max(scores, axis=2)
    weights = jnp.where(valid_mask, jnp.exp(scores - local_max[:, :, None]), 0.0)
    local_total = jnp.sum(weights, axis=2)
    local_out = jnp.einsum(
        "shc,scl->shl",
        weights.astype(jnp.bfloat16),
        latent_cache[:, :, :LAT],
        preferred_element_type=jnp.float32,
    )
    out_rows = out_proj.shape[0]
    col_count = H * LAT // kv_count
    segment = min(col_count, LAT)
    head_count = col_count // segment
    head_start = shard_index * col_count // LAT
    global_max = lax.pmax(local_max, "kv")
    scaling = jnp.exp(local_max - global_max)
    weight_total = lax.psum(local_total * scaling, "kv")
    scaled = (local_out * scaling[:, :, None]).reshape(seq_count, H * LAT)
    merged_sum = lax.psum_scatter(scaled, "kv", scatter_dimension=1, tiled=True).reshape(
        seq_count, head_count, segment
    )
    own_total = lax.dynamic_slice_in_dim(weight_total, head_start, head_count, 1)
    merged = merged_sum / own_total[:, :, None]
    projector = value_up.reshape(head_count, segment, VD).astype(jnp.float32)
    value_part = jnp.einsum("shl,hlv->shv", merged, projector, precision=lax.Precision.HIGHEST)
    holders = kv_count // H if kv_count > H else 1
    for bit in range(holders.bit_length() - 1):
        value_part = value_part + from_partner(value_part, "kv", bit)
    value_rows = value_part.astype(jnp.bfloat16).reshape(seq_count, head_count * VD)
    if holders > 1:
        value_rows = lax.dynamic_slice_in_dim(
            value_rows, shard_index % holders * out_rows, out_rows, 1
        )
    partial_out = jnp.dot(value_rows, out_proj, preferred_element_type=jnp.float32)
    experts_local = EXPERTS // kv_count
    slot_count = experts_local * CAP
    targets = slot_targets(expert_ids)
    own_match = slot_match(targets, shard_index * slot_count, slot_count)
    own_pick = token_picker(own_match, seq_count)
    slot_gate = jnp.dot(own_match, gate_weights.reshape(-1), precision=lax.Precision.HIGHEST)
    attn_rows = lax.psum(partial_out, "kv")
    resid_rows, gain_cols = (
        lax.all_gather(residual, "kv", axis=1, tiled=True),
        lax.all_gather(norm_gain, "kv", axis=0, tiled=True),
    )
    summed = attn_rows + resid_rows.astype(jnp.float32)
    inverse_rms = lax.rsqrt(jnp.mean(summed * summed, axis=1) + small_eps)
    normed = summed * inverse_rms[:, None] * gain_cols.astype(jnp.float32)
    peak_abs = jnp.max(jnp.abs(normed), axis=1) + small_eps
    coded_rows = (normed / peak_abs[:, None]).astype(jnp.bfloat16)
    dispatched = jnp.dot(
        own_pick.astype(jnp.bfloat16), coded_rows, preferred_element_type=jnp.float32
    ).astype(jnp.bfloat16)
    slot_scale = jnp.dot(own_pick, peak_abs, precision=lax.Precision.HIGHEST)
    return (
        dispatched.reshape(experts_local, CAP, D),
        slot_scale.reshape(experts_local, CAP),
        slot_gate.reshape(experts_local, CAP),
    )


def solution(mesh):
    in_specs = (
        P("groups", "kv"),
        P("groups", "kv", None),
        P("groups"),
        P("kv", None),
        P("kv", None),
        P("groups", "kv"),
        P("kv"),
        P("groups", None),
        P("groups", None),
    )
    out_specs = (
        P(("groups", "kv"), None, None),
        P(("groups", "kv"), None),
        P(("groups", "kv"), None),
    )
    return jax.shard_map(
        per_device, mesh=mesh, in_specs=in_specs, out_specs=out_specs, check_vma=False
    )
```

profile of v0, /device:TPU:0, one launch (start us, length us, event | category | flops | bytes accessed | tf_op | source)
XLA Modules:
  0.0 314.2 jit_solution(11004834008479304627)
XLA Ops:
  7.2 0.0 copy-start
  7.2 0.0 all-gather.3.cloned.1.call-start
  7.2 0.7 all-gather.3.cloned.1.call-update
  7.9 0.0 reduce-scatter.2.cloned.1.call-start
  8.0 0.7 broadcast_compare_fusion.1
  8.7 43.6 %all-gather.3.cloned.1.call-done = bf16[40,18432]{1,0:T(8,128)(2,1)} async-done(((bf16[40,1152]{1,0:T(8,128)(2,1)}), bf16[40,18432]{1,0:T(8,128)(2,1)}) %all-gather.3.cloned.1.call-update) | async-done | bytes 1474576 | tf_op jit(solution)/shard_map/all_gather | solution.py:58
  52.3 3.3 %reshape.111 = bf16[40,32,576]{2,1,0:T(8,128)(2,1)S(1)} reshape(bf16[40,18432]{1,0:T(8,128)(2,1)} %all-gather.3.cloned.1.call-done) | data formatting | bytes 2949120 | tf_op jit(solution)/shard_map/reshape | solution.py:58
  55.5 3.9 %fusion.26 = (f32[40,32]{1,0:T(8,128)S(1)}, f32[40,32,128]{2,1,0:T(8,128)S(1)}) fusion(bf16[40,32,576]{2,1,0:T(8,128)(2,1)S(1)} %reshape.111, bf16[40,128,576]{1,2,0:T(8,128)(2,1)} %param.10, pred[40,128]{1,0:T(8,128)(4,1)S(1)} %broadcast_compare_fusion.1), kind=kOutput, calls=%fused_computation.47 | convolution fusion | flops 189233920 | bytes 8038400 | tf_op jit(solution)/shard_map/shq,scq->shc/dot_general | solution.py:61
  59.4 59.5 %pmax.7 = f32[40,32]{1,0:T(8,128)S(1)} all-reduce(f32[40,32]{1,0:T(8,128)S(1)} %get-tuple-element.5), channel_id=1, replica_groups=mesh['groups'=2,'kv'=16] {'kv'}, use_global_device_ids=true, to_apply=%region_3.4 | all-reduce | flops 1280 | bytes 10240 | tf_op jit(solution)/shard_map/pmax | solution.py:81
  118.9 0.4 fusion.7
  119.4 3.9 %fusion.2 = f32[40,32,512]{2,1,0:T(8,128)S(1)} fusion(bf16[40,128,576]{1,2,0:T(8,128)(2,1)} %param.10, f32[40,32]{1,0:T(8,128)S(1)} %get-tuple-element.4, f32[40,32,128]{2,1,0:T(8,128)S(1)} %get-tuple-element.6, f32[40,32]{1,0:T(8,128)S(1)} %get-tuple-element.5, pred[40,128]{1,0:T(8,128)(4,1)S(1)} %broadcast_compare_fusion.1), kind=kOutput, calls=%fused_computation.3 | convolution fusion | flops 168919040 | bytes 8535040 | tf_op jit(solution)/shard_map/shc,scl->shl/dot_general | solution.py:70
  123.3 3.0 copy.51
  126.3 0.0 reduce-scatter.2.cloned.1.call-update
  126.3 0.0 all-reduce.3.cloned.1.call-start
  126.4 0.6 copy-done.3
  127.0 0.1 copy.38
  127.1 0.1 eq.41
  127.2 0.2 convert_reduce_fusion
  127.4 0.1 reduce_sum.39
  127.5 0.1 copy.39
  127.6 19.1 %all-gather = bf16[16,448,40]{1,2,0:T(8,128)(2,1)S(1)} all-gather(bf16[1,448,40]{1,2,0:T(8,128)(2,1)S(1)} %bitcast.43), channel_id=1, replica_groups=mesh['groups'=2,'kv'=16] {'kv'}, dimensions={0}, use_global_device_ids=true | all-gather | bytes 609280 | tf_op jit(solution)/shard_map/all_gather | solution.py:109
  146.7 59.9 %psum.14 = f32[40,32]{1,0:T(8,128)S(1)} all-reduce(f32[40,32]{1,0:T(8,128)S(1)} %get-tuple-element.3), channel_id=1, replica_groups=mesh['groups'=2,'kv'=16] {'kv'}, use_global_device_ids=true, to_apply=%region_6.7 | all-reduce | flops 1280 | bytes 10240 | tf_op jit(solution)/shard_map/psum | solution.py:83
  206.7 0.1 constant_dynamic-slice_fusion
  206.7 1.1 reshape.113
  207.8 0.1 broadcast_divide_fusion
  207.9 0.2 fusion.6
  208.2 3.8 %fusion.17 = f32[40,7168]{1,0:T(8,128)} fusion(bf16[256,7168]{1,0:T(8,128)(2,1)} %param.13, bf16[2,5,8,128]{3,2,1,0:T(8,128)(2,1)S(1)} %fusion.6), kind=kOutput, calls=%fused_computation.28 | convolution fusion | flops 146800640 | bytes 4837376 | tf_op jit(solution)/shard_map/dot_general | solution.py:100
  212.0 0.0 all-reduce.3.cloned.1.call-update
  212.1 0.2 copy.43
  212.3 0.0 copy-start.6
  212.3 0.0 copy-start.5
  212.3 0.5 reshape.125
  212.9 0.1 copy-done.6
  212.9 0.6 dynamic-slice
  214.2 0.3 dynamic-update-slice
  214.4 57.8 %all-reduce = bf16[7168]{0:T(1024)(128)(2,1)S(1)} all-reduce(bf16[7168]{0:T(1024)(128)(2,1)S(1)} %dynamic-update-slice), channel_id=1, replica_groups=mesh['groups'=2,'kv'=16] {'kv'}, use_global_device_ids=true, to_apply=%add | all-reduce | flops 7168 | bytes 28672
  272.3 0.1 copy.44
  272.3 0.1 reshape.128
  272.4 0.1 convert_reduce_fusion.1
  272.6 0.1 broadcast_compare_fusion
  272.7 0.8 fusion.15
  273.5 30.1 %all-reduce.3.cloned.1.call-done = f32[40,7168]{1,0:T(8,128)} async-done(((f32[40,7168]{1,0:T(8,128)}), f32[40,7168]{1,0:T(8,128)}) %all-reduce.3.cloned.1.call-update) | async-done | bytes 1146896 | tf_op jit(solution)/shard_map/psum | solution.py:107
  303.6 1.6 multiply_reduce_fusion
  305.1 0.0 copy-done.1
  305.2 0.4 abs_reduce_fusion
  305.5 0.4 convolution_convert_fusion
  306.0 0.9 reshape.116
  306.9 0.8 fusion.20
  (19 shorter events, 0.1 us)
Async XLA Ops:
  7.2 200.8 %copy-start = (bf16[1024,128]{1,0:T(8,128)(2,1)S(1)}, bf16[1024,128]{1,0:T(8,128)(2,1)}, u32[]{:S(2)}) copy-start(bf16[1024,128]{1,0:T(8,128)(2,1)} %param.12) | copy-start | bytes 786436
  7.2 45.1 %all-gather.3.cloned.1.call-start = ((), (), s32[]{:S(2)}) async-start(), calls=%async_computation.1 | async-start | bytes 1566720 | tf_op jit(solution)/shard_map/all_gather | solution.py:58
  7.9 198.8 %reduce-scatter.2.cloned.1.call-start = ((), (), s32[]{:S(2)}) async-start(), calls=%async_computation.2 | async-start | bytes 2785280 | tf_op jit(solution)/shard_map/reduce_scatter | solution.py:85
  126.3 0.7 copy-start.3
  126.3 1.3 copy-start.2
  126.3 177.2 %all-reduce.3.cloned.1.call-start = ((), (), s32[]{:S(2)}) async-start(), calls=%async_computation.3 | async-start | bytes 2293760 | tf_op jit(solution)/shard_map/psum | solution.py:107
  212.3 0.7 copy-start.6
  212.3 1.9 copy-start.5
  212.3 60.0 %copy-start.4 = (f32[40,8]{0,1:T(8,128)S(1)}, f32[40,8]{0,1:T(8,128)}, u32[]{:S(2)}) copy-start(f32[40,8]{0,1:T(8,128)} %param.17) | copy-start | bytes 3844
  303.6 1.6 copy-start.1
Sparse Core Ops, SparseCore 0:
  10.2 42.0 all-gather.2
  126.5 61.4 reduce-scatter.1
  212.2 91.3 all-reduce.2
where the time goes:
time: 315 us; the launch traced here: 314 us
  blocking collectives  196 us (62%)
  waiting for transfers between devices  74.4 us (24%)
  between operations  14.6 us (5%)
  matrix products  13.9 us (4%)
  local copies, waits for them, and re-layouts  11.1 us (4%)
  other arithmetic  3.74 us (1%)
    psum x1, blocking collectives, per_device(): weight_total = lax.psum(local_total * scaling, 'kv')  59.9 us
    pmax x1, blocking collectives, per_device(): global_max = lax.pmax(local_max, 'kv')  59.5 us
    unnamed x1, blocking collectives  57.8 us
    all_gather x1, waiting for transfers between devices, per_device(): lax.all_gather(queries, 'kv', axis=1, tiled=True)  43.6 us
    psum x1, waiting for transfers between devices, per_device(): attn_rows = lax.psum(partial_out, 'kv')  30.1 us
    all_gather x1, blocking collectives, per_device(): lax.all_gather(residual, 'kv', axis=1, tiled=True)  19.1 us
  transfers between devices with their start and end apart: 3, of which 2 were waited for; matrix products, arithmetic and copies ran while one was open for 1% of the time, Pallas kernels for 0%

commit v1 on v0

--- a/solution.py
+++ b/solution.py
@@ -104,7 +104,23 @@
     own_match = slot_match(targets, shard_index * slot_count, slot_count)
     own_pick = token_picker(own_match, seq_count)
     slot_gate = jnp.dot(own_match, gate_weights.reshape(-1), precision=lax.Precision.HIGHEST)
-    attn_rows = lax.psum(partial_out, "kv")
+
+    def find_limits(z):
+        shard_axis = "kv"
+        fan = lax.axis_size(shard_axis)
+
+        def read_spans(b_now, r1):
+            if r1 >= fan:
+                return b_now
+            return read_spans(
+                b_now
+                + lax.ppermute(b_now, shard_axis, perm=tuple(((i0, i0 ^ r1) for i0 in range(fan)))),
+                2 * r1,
+            )
+
+        return read_spans(z, 1)
+
+    attn_rows = find_limits(partial_out)
     resid_rows, gain_cols = (
         lax.all_gather(residual, "kv", axis=1, tiled=True),
         lax.all_gather(norm_gain, "kv", axis=0, tiled=True),

time: 315 us -> 369 us (1.17)
  blocking collectives: 196 us -> 245 us
    psum x1 -> x0, waiting for transfers between devices: 30.1 us -> none  [per_device(): attn_rows = lax.psum(partial_out, 'kv')]
    ppermute x0 -> x4, waiting for transfers between devices: none -> 29.1 us  [read_spans(): lax.ppermute(b_now, shard_axis, perm=tuple(((i0, i0 ^ r1) for i0 in range...]
    unnamed x1, blocking collectives: 57.8 us -> 86.5 us
    all_gather x1, blocking collectives: 19.1 us -> 41.2 us  [per_device(): lax.all_gather(residual, 'kv', axis=1, tiled=True)]
  transfers between devices with their start and end apart: 3 -> 6, of which waited for: 2 -> 4; matrix products, arithmetic and copies ran while one was open for 1% -> 1% of each run, Pallas kernels for 0% -> 0%
where the time goes in v1:
time: 369 us; the launch traced here: 368 us
  blocking collectives  245 us (66%)
  waiting for transfers between devices  76.8 us (21%)
  between operations  14.9 us (4%)
  matrix products  12.8 us (3%)
  local copies, waits for them, and re-layouts  10.5 us (3%)
  other arithmetic  5.31 us (1%)
    unnamed x1, blocking collectives  86.5 us
    pmax x1, blocking collectives, per_device(): global_max = lax.pmax(local_max, 'kv')  59.5 us
    psum x1, blocking collectives, per_device(): weight_total = lax.psum(local_total * scaling, 'kv')  58.2 us
    all_gather x1, waiting for transfers between devices, per_device(): lax.all_gather(queries, 'kv', axis=1, tiled=True)  43.6 us
    all_gather x1, blocking collectives, per_device(): lax.all_gather(residual, 'kv', axis=1, tiled=True)  41.2 us
    ppermute x4, waiting for transfers between devices, read_spans(): lax.ppermute(b_now, shard_axis, perm=tuple(((i0, i0 ^ r1) for i0 in range...  29.1 us
  transfers between devices with their start and end apart: 6, of which 4 were waited for; matrix products, arithmetic and copies ran while one was open for 1% of the time, Pallas kernels for 0%

profile of v1, /device:TPU:0, one launch (start us, length us, event | category | flops | bytes accessed | tf_op | source)
XLA Modules:
  0.0 368.2 jit_solution(16339214425957454617)
XLA Ops:
  7.2 0.0 all-gather.3.cloned.1.call-start
  7.2 0.7 all-gather.3.cloned.1.call-update
  7.9 0.0 reduce-scatter.2.cloned.1.call-start
  8.0 0.7 broadcast_compare_fusion.1
  8.7 43.6 %all-gather.3.cloned.1.call-done = bf16[40,18432]{1,0:T(8,128)(2,1)} async-done(((bf16[40,1152]{1,0:T(8,128)(2,1)}), bf16[40,18432]{1,0:T(8,128)(2,1)}) %all-gather.3.cloned.1.call-update) | async-done | bytes 1474576 | tf_op jit(solution)/shard_map/all_gather | solution.py:58
  52.3 3.3 reshape.111
  55.5 3.9 %fusion.26 = (f32[40,32]{1,0:T(8,128)S(1)}, f32[40,32,128]{2,1,0:T(8,128)S(1)}) fusion(bf16[40,32,576]{2,1,0:T(8,128)(2,1)S(1)} %reshape.111, bf16[40,128,576]{1,2,0:T(8,128)(2,1)} %param.10, pred[40,128]{1,0:T(8,128)(4,1)S(1)} %broadcast_compare_fusion.1), kind=kOutput, calls=%fused_computation.47 | convolution fusion | flops 189233920 | bytes 8038400 | tf_op jit(solution)/shard_map/shq,scq->shc/dot_general | solution.py:61
  59.4 59.5 %pmax.7 = f32[40,32]{1,0:T(8,128)S(1)} all-reduce(f32[40,32]{1,0:T(8,128)S(1)} %get-tuple-element.7), channel_id=1, replica_groups=mesh['groups'=2,'kv'=16] {'kv'}, use_global_device_ids=true, to_apply=%region_3.4 | all-reduce | flops 1280 | bytes 10240 | tf_op jit(solution)/shard_map/pmax | solution.py:81
  118.9 0.4 fusion.7
  119.4 3.9 %fusion.2 = f32[40,32,512]{2,1,0:T(8,128)S(1)} fusion(bf16[40,128,576]{1,2,0:T(8,128)(2,1)} %param.10, f32[40,32]{1,0:T(8,128)S(1)} %get-tuple-element.6, f32[40,32,128]{2,1,0:T(8,128)S(1)} %get-tuple-element.8, f32[40,32]{1,0:T(8,128)S(1)} %get-tuple-element.7, pred[40,128]{1,0:T(8,128)(4,1)S(1)} %broadcast_compare_fusion.1), kind=kOutput, calls=%fused_computation.3 | convolution fusion | flops 168919040 | bytes 8535040 | tf_op jit(solution)/shard_map/shc,scl->shl/dot_general | solution.py:70
  123.3 3.0 copy.51
  126.3 58.2 %psum.7 = f32[40,32]{1,0:T(8,128)S(1)} all-reduce(f32[40,32]{1,0:T(8,128)S(1)} %get-tuple-element.5), channel_id=1, replica_groups=mesh['groups'=2,'kv'=16] {'kv'}, use_global_device_ids=true, to_apply=%region_6.7 | all-reduce | flops 1280 | bytes 10240 | tf_op jit(solution)/shard_map/psum | solution.py:83
  184.5 0.1 constant_dynamic-slice_fusion
  184.6 3.5 reduce-scatter.2.cloned.1.call-done
  188.1 1.1 reshape.113
  189.1 0.1 broadcast_divide_fusion
  189.3 0.2 fusion.6
  189.5 2.8 fusion.17
  192.3 0.1 collective-permute-start
  192.4 2.8 collective-permute-done
  195.1 0.1 add.79
  195.3 1.1 collective-permute-start.1
  196.4 26.3 %collective-permute-done.1 = f32[40,7168]{1,0:T(8,128)S(1)} collective-permute-done((f32[40,7168]{1,0:T(8,128)S(1)}, f32[40,7168]{1,0:T(8,128)S(1)}, u32[]{:S(2)}, u32[]{:S(2)}) %collective-permute-start.1) | collective-permute-done | bytes 1146912 | tf_op jit(solution)/shard_map/ppermute | solution.py:117
  222.7 0.1 add.80
  222.8 1.3 collective-permute-start.2
  224.0 0.1 copy.38
  224.1 0.1 eq.41
  224.2 0.2 convert_reduce_fusion
  224.4 41.2 %all-gather = bf16[16,448,40]{1,2,0:T(8,128)(2,1)S(1)} all-gather(bf16[1,448,40]{1,2,0:T(8,128)(2,1)S(1)} %bitcast.37), channel_id=1, replica_groups=mesh['groups'=2,'kv'=16] {'kv'}, dimensions={0}, use_global_device_ids=true | all-gather | bytes 609280 | tf_op jit(solution)/shard_map/all_gather | solution.py:125
  265.6 1.1 add.81
  266.7 0.2 copy.43
  267.0 0.5 reshape.125
  267.5 0.1 copy-done.5
  267.6 0.6 dynamic-slice
  268.9 0.3 dynamic-update-slice
  269.1 86.5 %all-reduce = bf16[7168]{0:T(1024)(128)(2,1)S(1)} all-reduce(bf16[7168]{0:T(1024)(128)(2,1)S(1)} %dynamic-update-slice), channel_id=1, replica_groups=mesh['groups'=2,'kv'=16] {'kv'}, use_global_device_ids=true, to_apply=%add | all-reduce | flops 7168 | bytes 28672
  355.6 0.1 reduce_sum.39
  355.7 0.1 copy.39
  355.8 0.1 copy.44
  355.8 0.1 reshape.128
  356.0 0.1 convert_reduce_fusion.1
  356.1 0.1 broadcast_compare_fusion
  356.2 0.8 fusion.15
  357.0 1.9 multiply_reduce_fusion
  358.9 0.3 abs_reduce_fusion
  359.2 0.4 convolution_convert_fusion
  359.6 0.9 reshape.116
  360.6 0.8 fusion.20
  (25 shorter events, 0.1 us)
Async XLA Ops:
  7.2 182.1 %copy-start = (bf16[1024,128]{1,0:T(8,128)(2,1)S(1)}, bf16[1024,128]{1,0:T(8,128)(2,1)}, u32[]{:S(2)}) copy-start(bf16[1024,128]{1,0:T(8,128)(2,1)} %param.12) | copy-start | bytes 786436
  7.2 45.1 %all-gather.3.cloned.1.call-start = ((), (), s32[]{:S(2)}) async-start(), calls=%async_computation.1 | async-start | bytes 1566720 | tf_op jit(solution)/shard_map/all_gather | solution.py:58
  7.9 180.2 %reduce-scatter.2.cloned.1.call-start = ((), (), s32[]{:S(2)}) async-start(), calls=%async_computation.2 | async-start | bytes 2785280 | tf_op jit(solution)/shard_map/reduce_scatter | solution.py:85
  192.3 2.9 collective-permute-start
  195.3 28.8 %copy-start.2 = (s32[40,8]{0,1:T(8,128)S(1)}, s32[40,8]{0,1:T(8,128)}, u32[]{:S(2)}) copy-start(s32[40,8]{0,1:T(8,128)} %param.16) | copy-start | bytes 3844
  195.3 29.2 %copy-start.1 = (bf16[40,448]{1,0:T(8,128)(2,1)S(1)}, bf16[40,448]{1,0:T(8,128)(2,1)}, u32[]{:S(2)}) copy-start(bf16[40,448]{1,0:T(8,128)(2,1)} %param.14) | copy-start | bytes 107524
  195.3 27.4 %collective-permute-start.1 = (f32[40,7168]{1,0:T(8,128)S(1)}, f32[40,7168]{1,0:T(8,128)S(1)}, u32[]{:S(2)}, u32[]{:S(2)}) collective-permute-start(f32[40,7168]{1,0:T(8,128)S(1)} %add.79), channel_id=1, source_target_pairs={{0,2},{1,3},{2,0},{3,1},{4,6},{5,7},{6,4},{7,5},{8,10},{9,11},{10,... | collective-permute-start | bytes 3440648 | tf_op jit(solution)/shard_map/ppermute | solution.py:117
  222.8 42.8 %collective-permute-start.2 = (f32[40,7168]{1,0:T(8,128)S(1)}, f32[40,7168]{1,0:T(8,128)S(1)}, u32[]{:S(2)}, u32[]{:S(2)}) collective-permute-start(f32[40,7168]{1,0:T(8,128)S(1)} %add.80), channel_id=1, source_target_pairs={{0,4},{1,5},{2,6},{3,7},{4,0},{5,1},{6,2},{7,3},{8,12},{9,13},{10,... | collective-permute-start | bytes 3440648 | tf_op jit(solution)/shard_map/ppermute | solution.py:117
  266.7 90.3 %collective-permute-start.3 = (f32[40,7168]{1,0:T(8,128)}, f32[40,7168]{1,0:T(8,128)}, u32[]{:S(2)}, u32[]{:S(2)}) collective-permute-start(f32[40,7168]{1,0:T(8,128)} %add.81), channel_id=1, source_target_pairs={{0,8},{1,9},{2,10},{3,11},{4,12},{5,13},{6,14},{7,15},{8,0},{9,1},... | collective-permute-start | bytes 3440648 | tf_op jit(solution)/shard_map/ppermute | solution.py:117
  267.0 0.7 copy-start.5
  267.0 1.9 copy-start.4
  267.0 88.8 %copy-start.3 = (f32[40,8]{0,1:T(8,128)S(1)}, f32[40,8]{0,1:T(8,128)}, u32[]{:S(2)}) copy-start(f32[40,8]{0,1:T(8,128)} %param.17) | copy-start | bytes 3844
Sparse Core Ops, SparseCore 0:
  10.2 42.0 all-gather.2
  126.5 61.5 reduce-scatter.1
